TPU v7x, 32 devices: a whole 2x2x4 slice. The times are simulated.
32 devices in a mesh: leaf: 8 (over z, x), rows: 4 (over y, core).
Axes of the slice: x: 2, y: 2, z: 4, core: 2. Of those that a mesh axis runs over, the one named last changes fastest.
Arguments:
- right_side: float32 [8, 32768], P(None, ('leaf', 'rows')), may hold values from -6 to 6
- diagonal: float32 [32768], P(('leaf', 'rows')), may hold values from 0.5 to 4
- tree_order: int32 [32768], P(('leaf', 'rows')), may hold values from 0 to 32767, as said below
- mid_perm: int32 [8], replicated, may hold values from 0 to 7, each once
- col_factor: bfloat16 [32768, 384], P(('leaf', 'rows')), may hold values from -0.1875 to 0.1875
- mid_factor: bfloat16 [3072, 768], P('leaf', 'rows'), may hold values from -0.15625 to 0.15625
- pre_factor: bfloat16 [3072, 768], P('leaf', 'rows'), may hold values from -0.15625 to 0.15625
- row_factor: bfloat16 [48, 32768], P(None, ('leaf', 'rows')), may hold values from -0.875 to 0.875
Outputs:
- solution: float32 [8, 32768], P(None, ('leaf', 'rows'))
- residual: float32 [8, 32768], P(None, ('leaf', 'rows'))
Inputs may be any that keep to these rules, and one draw needn't show every extreme that they name: `tree_order`: each aligned run of 1024 entries, the run starting at b * 1024, is a permutation of b * 1024 to (b + 1) * 1024 - 1. `mid_perm`: a permutation of 0 to 7.
All inputs are finite; a program needn't handle non-finite values.
Results may differ from a plain program's by a relative error of at most 0.025.
Values may be sent and summed in bfloat16 or wider, within the bound.
No kernel may reach another device: no remote copies, remote signals or barrier semaphores. Data moves between devices by JAX's collectives and lax.ppermute only.
A program may use at most 64 MiB of HBM per device.

v0:
```python
import jax
import jax.numpy as jnp
from jax import lax
from jax.sharding import PartitionSpec as P

ITERS = 2


def curvature(first, second):
    return lax.psum(jnp.sum(first * second, axis=1), ("leaf", "rows"))


def precond_norm(first, second):
    return lax.psum(jnp.sum(first * second, axis=1), ("leaf", "rows"))


def per_device(
    right_side, diagonal, tree_order, mid_perm, col_factor, mid_factor, pre_factor, row_factor
):
    sides, points = right_side.shape
    rank_size = row_factor.shape[0]
    leaves = mid_perm.shape[0]
    row_count = mid_factor.shape[1] // rank_size
    local_index = tree_order % points
    slot_ids = jnp.arange(leaves, dtype=jnp.int32)
    onehot = (mid_perm[:, None] == slot_ids[None, :]).astype(jnp.bfloat16)
    col_split = col_factor.reshape(points, leaves, rank_size)
    own_gram = jnp.dot(row_factor, row_factor.T, preferred_element_type=jnp.float32)
    gram_blocks = lax.all_gather(own_gram[None], "rows", axis=0, tiled=True)

    def gram_apply(field, mid_weight):
        taken_tree = jnp.take(field, local_index, axis=1).astype(jnp.bfloat16)
        coeffs = jnp.einsum(
            "sn,ngk->gsk", taken_tree, col_split, preferred_element_type=jnp.float32
        ).astype(jnp.bfloat16)
        outgoing = jnp.einsum(
            "qg,gsk->qsk", onehot, coeffs, preferred_element_type=jnp.float32
        ).astype(jnp.bfloat16)
        incoming = lax.all_to_all(
            outgoing.reshape(leaves, sides * rank_size),
            "leaf",
            split_axis=0,
            concat_axis=0,
            tiled=True,
        )
        incoming = incoming.reshape(leaves, sides, rank_size)
        weight_split = mid_weight.reshape(leaves, rank_size, row_count * rank_size)
        partial_value = jnp.einsum(
            "lsk,lkm->sm", incoming, weight_split, preferred_element_type=jnp.float32
        )
        totals = lax.psum(partial_value, "rows")
        head_coef = lax.optimization_barrier(totals.astype(jnp.bfloat16)).astype(jnp.float32)
        head_coef = head_coef.reshape(sides, row_count, rank_size)
        gathered = jnp.einsum(
            "sjk,jkm->sjm", head_coef, gram_blocks, precision=lax.Precision.HIGHEST
        )
        gathered = gathered.reshape(sides, row_count * rank_size).astype(jnp.bfloat16)
        returned = jnp.einsum(
            "sm,lkm->lsk", gathered, weight_split, preferred_element_type=jnp.float32
        ).astype(jnp.bfloat16)
        arrived = lax.all_to_all(
            returned.reshape(leaves, sides * rank_size),
            "leaf",
            split_axis=0,
            concat_axis=0,
            tiled=True,
        )
        arrived = arrived.reshape(leaves, sides, rank_size)
        unsent = jnp.einsum(
            "qg,qsk->gsk", onehot, arrived, preferred_element_type=jnp.float32
        ).astype(jnp.bfloat16)
        tree_out = jnp.einsum("gsk,ngk->sn", unsent, col_split, preferred_element_type=jnp.float32)
        return jnp.zeros_like(tree_out).at[:, local_index].set(tree_out)

    def apply_precond(field):
        return field / diagonal[None, :] + gram_apply(field, pre_factor)

    solution = jnp.zeros_like(right_side)
    residual = right_side
    precond = apply_precond(residual)
    direction = precond
    precond_dot = precond_norm(residual, precond)
    for iteration in range(ITERS):
        image = diagonal[None, :] * direction + gram_apply(direction, mid_factor)
        alpha_step = precond_dot / curvature(direction, image)
        solution = solution + alpha_step[:, None] * direction
        residual = residual - alpha_step[:, None] * image
        if iteration + 1 < ITERS:
            precond = apply_precond(residual)
            dot_next = precond_norm(residual, precond)
            direction = precond + (dot_next / precond_dot)[:, None] * direction
            precond_dot = dot_next
    return (solution, residual)


def solution(mesh):
    return jax.shard_map(
        per_device,
        mesh=mesh,
        in_specs=(
            P(None, ("leaf", "rows")),
            P(("leaf", "rows")),
            P(("leaf", "rows")),
            P(),
            P(("leaf", "rows"), None),
            P("leaf", "rows"),
            P("leaf", "rows"),
            P(None, ("leaf", "rows")),
        ),
        out_specs=(P(None, ("leaf", "rows")), P(None, ("leaf", "rows"))),
        check_vma=False,
    )
```

profile of v0, /device:TPU:0, one launch (start us, length us, event | category | flops | bytes accessed | tf_op | source)
XLA Modules:
  0.0 275.6 jit_solution(600486382952462527)
XLA Ops:
  2.3 3.2 %gather_fusion = bf16[1024,8]{1,0:T(8,128)(2,1)S(1)} fusion(bf16[8,1024]{0,1:T(8,128)(2,1)S(1)} %copy.167, s32[1024]{0:T(1024)S(1)} %broadcast_clamp_fusion), kind=kCustom, calls=%fused_computation.clone | custom fusion | bytes 36864 | tf_op jit(solution)/shard_map/jit(_take)/gather | solution.py:32
  9.9 7.3 %all-to-all-start = ((bf16[8,2,192]{2,1,0:T(2,128)(2,1)}), bf16[8,2,192]{2,1,0:T(2,128)(2,1)S(1)}, u32[]{:S(2)}, u32[]{:S(2)}) async-start(bf16[8,2,192]{2,1,0:T(2,128)(2,1)} %reshape.246), calls=%async_computation | async-start | bytes 16384 | tf_op jit(solution)/shard_map/all_to_all | solution.py:39
  17.5 5.3 %all-gather = f32[192,48]{1,0:T(8,128)S(1)} all-gather(f32[48,48]{1,0:T(8,128)S(1)} %fusion.74), channel_id=2, replica_groups=mesh['leaf'=8,'rows'=4] {'rows'}, dimensions={0}, use_global_device_ids=true | all-gather | bytes 46080 | tf_op jit(solution)/shard_map/all_gather | solution.py:29
  24.1 6.3 %psum.56 = bf16[8,192]{1,0:T(8,128)(2,1)S(1)} all-reduce(f32[8,192]{1,0:T(8,128)S(1)} %convolution_bitcast_fusion.7), channel_id=1, replica_groups=mesh['leaf'=8,'rows'=4] {'rows'}, use_global_device_ids=true, to_apply=%region_0.2 | all-reduce | flops 1536 | bytes 9216 | tf_op jit(solution)/shard_map/psum | solution.py:51
  31.9 12.3 %all_to_all.80 = bf16[8,2,192]{2,1,0:T(2,128)(2,1)S(1)} all-to-all(bf16[8,2,192]{2,1,0:T(2,128)(2,1)S(1)} %reshape.248), channel_id=1, replica_groups=mesh['leaf'=8,'rows'=4] {'leaf'}, dimensions={0} | all-to-all | bytes 12288 | tf_op jit(solution)/shard_map/all_to_all | solution.py:61
  45.0 3.2 %scatter_custom_fusion = f32[8,1024]{0,1:T(8,128)S(1)} fusion(s32[1024]{0:T(1024)S(1)} %get-tuple-element.16, f32[1024,8]{1,0:T(8,128)S(1)} %copy.180, f32[]{:T(128)} %constant.15.clone.1), kind=kCustom, calls=%fused_computation.54 | custom fusion | bytes 32772 | tf_op jit(solution)/shard_map/scatter | solution.py:73
  49.2 3.2 %gather_fusion.1 = bf16[1024,8]{1,0:T(8,128)(2,1)S(1)} fusion(bf16[8,1024]{0,1:T(8,128)(2,1)S(1)} %copy.182, s32[1024]{0:T(1024)S(1)} %broadcast_clamp_fusion), kind=kCustom, calls=%fused_computation.1.clone | custom fusion | bytes 36864 | tf_op jit(solution)/shard_map/jit(_take)/gather | solution.py:32
  54.7 3.3 %all-to-all-start.2 = ((bf16[8,2,192]{2,1,0:T(2,128)(2,1)}), bf16[8,2,192]{2,1,0:T(2,128)(2,1)S(1)}, u32[]{:S(2)}, u32[]{:S(2)}) async-start(bf16[8,2,192]{2,1,0:T(2,128)(2,1)} %reshape.250), calls=%async_computation.2 | async-start | bytes 16384 | tf_op jit(solution)/shard_map/all_to_all | solution.py:39
  58.2 6.3 %all-to-all-done.2 = bf16[8,2,192]{2,1,0:T(2,128)(2,1)S(1)} async-done(((bf16[8,2,192]{2,1,0:T(2,128)(2,1)}), bf16[8,2,192]{2,1,0:T(2,128)(2,1)S(1)}, u32[]{:S(2)}, u32[]{:S(2)}) %all-to-all-start.2) | async-done | bytes 6176 | tf_op jit(solution)/shard_map/all_to_all | solution.py:39
  64.9 6.0 %psum.58 = bf16[8,192]{1,0:T(8,128)(2,1)S(1)} all-reduce(f32[8,192]{1,0:T(8,128)S(1)} %convolution_bitcast_fusion.6), channel_id=1, replica_groups=mesh['leaf'=8,'rows'=4] {'rows'}, use_global_device_ids=true, to_apply=%region_4.6 | all-reduce | flops 1536 | bytes 9216 | tf_op jit(solution)/shard_map/psum | solution.py:51
  72.3 8.9 %all_to_all.81 = bf16[8,2,192]{2,1,0:T(2,128)(2,1)S(1)} all-to-all(bf16[8,2,192]{2,1,0:T(2,128)(2,1)S(1)} %reshape.252), channel_id=1, replica_groups=mesh['leaf'=8,'rows'=4] {'leaf'}, dimensions={0} | all-to-all | bytes 12288 | tf_op jit(solution)/shard_map/all_to_all | solution.py:61
  82.0 3.2 %scatter_custom_fusion.1 = f32[8,1024]{0,1:T(8,128)S(1)} fusion(s32[1024]{0:T(1024)S(1)} %get-tuple-element.16, f32[1024,8]{1,0:T(8,128)S(1)} %copy.194, f32[]{:T(128)} %constant.15.clone.1), kind=kCustom, calls=%fused_computation.52 | custom fusion | bytes 32772 | tf_op jit(solution)/shard_map/scatter | solution.py:73
  85.6 38.2 %all-reduce = (f32[8]{0:T(128)S(1)}, f32[8]{0:T(128)S(1)}) all-reduce(f32[8]{0:T(128)S(1)} %get-tuple-element.12, f32[8]{0:T(128)S(1)} %get-tuple-element.11), channel_id=1, replica_groups=mesh['leaf'=8,'rows'=4] {'leaf','rows'}, use_global_device_ids=true, to_apply=%region_3.5 | all-reduce | flops 16 | bytes 128 | tf_op jit(solution)/shard_map/psum | solution.py:14
  124.1 3.2 %gather_fusion.2 = bf16[1024,8]{1,0:T(8,128)(2,1)S(1)} fusion(bf16[8,1024]{0,1:T(8,128)(2,1)S(1)} %copy.196, s32[1024]{0:T(1024)S(1)} %broadcast_clamp_fusion), kind=kCustom, calls=%fused_computation.2.clone | custom fusion | bytes 36864 | tf_op jit(solution)/shard_map/jit(_take)/gather | solution.py:32
  129.0 11.0 %all_to_all.82 = bf16[8,2,192]{2,1,0:T(2,128)(2,1)S(1)} all-to-all(bf16[8,2,192]{2,1,0:T(2,128)(2,1)S(1)} %reshape.254), channel_id=1, replica_groups=mesh['leaf'=8,'rows'=4] {'leaf'}, dimensions={0} | all-to-all | bytes 12288 | tf_op jit(solution)/shard_map/all_to_all | solution.py:39
  140.3 6.1 %psum.60 = bf16[8,192]{1,0:T(8,128)(2,1)S(1)} all-reduce(f32[8,192]{1,0:T(8,128)S(1)} %convolution_bitcast_fusion.5), channel_id=1, replica_groups=mesh['leaf'=8,'rows'=4] {'rows'}, use_global_device_ids=true, to_apply=%region_8.10 | all-reduce | flops 1536 | bytes 9216 | tf_op jit(solution)/shard_map/psum | solution.py:51
  147.9 8.9 %all_to_all.83 = bf16[8,2,192]{2,1,0:T(2,128)(2,1)S(1)} all-to-all(bf16[8,2,192]{2,1,0:T(2,128)(2,1)S(1)} %reshape.256), channel_id=1, replica_groups=mesh['leaf'=8,'rows'=4] {'leaf'}, dimensions={0} | all-to-all | bytes 12288 | tf_op jit(solution)/shard_map/all_to_all | solution.py:61
  157.6 3.4 %scatter_custom_fusion.2 = f32[8,1024]{0,1:T(8,128)S(1)} fusion(s32[1024]{0:T(1024)S(1)} %get-tuple-element.16, f32[1024,8]{1,0:T(8,128)S(1)} %copy.207, f32[]{:T(128)} %constant.15.clone.1), kind=kCustom, calls=%fused_computation.50 | custom fusion | bytes 32772 | tf_op jit(solution)/shard_map/scatter | solution.py:73
  161.3 38.2 %psum.61 = f32[8]{0:T(128)S(1)} all-reduce(f32[8]{0:T(128)S(1)} %multiply_reduce_fusion.1), channel_id=1, replica_groups=mesh['leaf'=8,'rows'=4] {'leaf','rows'}, use_global_device_ids=true, to_apply=%region_11.13 | all-reduce | flops 8 | bytes 64 | tf_op jit(solution)/shard_map/psum | solution.py:14
  204.6 11.0 %all_to_all.84 = bf16[8,2,192]{2,1,0:T(2,128)(2,1)S(1)} all-to-all(bf16[8,2,192]{2,1,0:T(2,128)(2,1)S(1)} %reshape.258), channel_id=1, replica_groups=mesh['leaf'=8,'rows'=4] {'leaf'}, dimensions={0} | all-to-all | bytes 12288 | tf_op jit(solution)/shard_map/all_to_all | solution.py:39
  216.0 6.1 %psum.62 = bf16[8,192]{1,0:T(8,128)(2,1)S(1)} all-reduce(f32[8,192]{1,0:T(8,128)S(1)} %convolution_bitcast_fusion.4), channel_id=1, replica_groups=mesh['leaf'=8,'rows'=4] {'rows'}, use_global_device_ids=true, to_apply=%region_12.14 | all-reduce | flops 1536 | bytes 9216 | tf_op jit(solution)/shard_map/psum | solution.py:51
  223.5 8.9 %all_to_all.85 = bf16[8,2,192]{2,1,0:T(2,128)(2,1)S(1)} all-to-all(bf16[8,2,192]{2,1,0:T(2,128)(2,1)S(1)} %reshape.260), channel_id=1, replica_groups=mesh['leaf'=8,'rows'=4] {'leaf'}, dimensions={0} | all-to-all | bytes 12288 | tf_op jit(solution)/shard_map/all_to_all | solution.py:61
  233.2 3.2 %scatter_custom_fusion.3 = f32[8,1024]{0,1:T(8,128)S(1)} fusion(s32[1024]{0:T(1024)S(1)} %get-tuple-element.16, f32[1024,8]{1,0:T(8,128)S(1)} %copy.220, f32[]{:T(128)} %constant.15.clone.1), kind=kCustom, calls=%fused_computation.48 | custom fusion | bytes 32772 | tf_op jit(solution)/shard_map/scatter | solution.py:73
  236.7 38.2 %psum.63 = f32[8]{0:T(128)S(1)} all-reduce(f32[8]{0:T(128)S(1)} %multiply_reduce_fusion), channel_id=1, replica_groups=mesh['leaf'=8,'rows'=4] {'leaf','rows'}, use_global_device_ids=true, to_apply=%region_15.17 | all-reduce | flops 8 | bytes 64 | tf_op jit(solution)/shard_map/psum | solution.py:10
  (139 shorter events, 29.8 us)
Async XLA Ops:
  0.6 16.6 %copy-start = (bf16[48,1024]{1,0:T(8,128)(2,1)S(1)}, bf16[48,1024]{1,0:T(8,128)(2,1)}, u32[]{:S(2)}) copy-start(bf16[48,1024]{1,0:T(8,128)(2,1)} %param.17) | copy-start | bytes 294916
  7.1 0.7 copy-start.5
  7.9 9.4 %copy-start.3 = (bf16[384,192]{0,1:T(8,128)(2,1)S(1)}, bf16[384,192]{0,1:T(8,128)(2,1)}, u32[]{:S(2)}) copy-start(bf16[384,192]{0,1:T(8,128)(2,1)} %param.16) | copy-start | bytes 442372
  9.9 13.8 %all-to-all-start = ((bf16[8,2,192]{2,1,0:T(2,128)(2,1)}), bf16[8,2,192]{2,1,0:T(2,128)(2,1)S(1)}, u32[]{:S(2)}, u32[]{:S(2)}) async-start(bf16[8,2,192]{2,1,0:T(2,128)(2,1)} %reshape.246), calls=%async_computation | async-start | bytes 16384 | tf_op jit(solution)/shard_map/all_to_all | solution.py:39
  48.3 0.8 copy-start.1
  48.3 0.8 copy-start.2
  52.5 5.5 %copy-start.4 = (bf16[384,192]{0,1:T(8,128)(2,1)S(1)}, bf16[384,192]{0,1:T(8,128)(2,1)}, u32[]{:S(2)}) copy-start(bf16[384,192]{0,1:T(8,128)(2,1)} %param.15) | copy-start | bytes 442372
  54.7 9.8 %all-to-all-start.2 = ((bf16[8,2,192]{2,1,0:T(2,128)(2,1)}), bf16[8,2,192]{2,1,0:T(2,128)(2,1)S(1)}, u32[]{:S(2)}, u32[]{:S(2)}) async-start(bf16[8,2,192]{2,1,0:T(2,128)(2,1)} %reshape.250), calls=%async_computation.2 | async-start | bytes 16384 | tf_op jit(solution)/shard_map/all_to_all | solution.py:39
where the time goes:
time: 277 us; the launch traced here: 276 us
  blocking collectives  205 us (74%)
  local copies, waits for them, and re-layouts  37.2 us (13%)
  starting transfers between devices  10.6 us (4%)
  other arithmetic  7.88 us (3%)
  waiting for transfers between devices  7.17 us (3%)
  matrix products  6.49 us (2%)
    psum x2, blocking collectives, precond_norm(): return lax.psum(jnp.sum(first * second, axis=1), ('leaf', 'rows'))  76.4 us
    all_to_all x4, blocking collectives, gram_apply(): lax.all_to_all(returned.reshape(leaves, sides * rank_size), 'leaf', split...  38.9 us
    psum x1, blocking collectives, curvature(): return lax.psum(jnp.sum(first * second, axis=1), ('leaf', 'rows'))  38.2 us
    psum x4, blocking collectives, gram_apply(): totals = lax.psum(partial_value, 'rows')  24.5 us
    all_to_all x2, blocking collectives, gram_apply(): lax.all_to_all(outgoing.reshape(leaves, sides * rank_size), 'leaf', split...  21.9 us
    scatter x8, local copies, waits for them, and re-layouts, gram_apply(): return jnp.zeros_like(tree_out).at[:, local_index].set(tree_out)  13.7 us
    gather x8, local copies, waits for them, and re-layouts, gram_apply(): taken_tree = jnp.take(field, local_index, axis=1).astype(jnp.bfloat16)  13.3 us
    all_to_all x2, starting transfers between devices, gram_apply(): lax.all_to_all(outgoing.reshape(leaves, sides * rank_size), 'leaf', split...  10.6 us
  transfers between devices with their start and end apart: 2, of which 2 were waited for; matrix products, arithmetic and copies ran while one was open for 0% of the time, Pallas kernels for 0%

commit v1 on v0

--- a/solution.py
+++ b/solution.py
@@ -11,7 +11,7 @@
 
 
 def precond_norm(first, second):
-    return lax.psum(jnp.sum(first * second, axis=1), ("leaf", "rows"))
+    return lax.psum(lax.psum(jnp.sum(first * second, axis=1), "rows"), "leaf")
 
 
 def per_device(

time: 277 us -> 284 us (1.025)
  blocking collectives: 205 us -> 212 us
    psum x1 -> x2, blocking collectives: 38.2 us -> 76.4 us  [curvature(): return lax.psum(jnp.sum(first * second, axis=1), ('leaf', 'rows'))]
    psum x2 -> x4, blocking collectives: 76.4 us -> 49.6 us  [precond_norm(): return lax.psum(lax.psum(jnp.sum(first * second, axis=1), 'rows'), 'leaf')]
    all_to_all x2, blocking collectives: 21.9 us -> 17.9 us  [gram_apply(): lax.all_to_all(outgoing.reshape(leaves, sides * rank_size), 'leaf', split...]
where the time goes in v1:
time: 284 us; the launch traced here: 283 us
  blocking collectives  212 us (75%)
  local copies, waits for them, and re-layouts  37 us (13%)
  starting transfers between devices  10.6 us (4%)
  other arithmetic  7.89 us (3%)
  waiting for transfers between devices  7.17 us (3%)
  matrix products  6.49 us (2%)
    psum x2, blocking collectives, curvature(): return lax.psum(jnp.sum(first * second, axis=1), ('leaf', 'rows'))  76.4 us
    psum x4, blocking collectives, precond_norm(): return lax.psum(lax.psum(jnp.sum(first * second, axis=1), 'rows'), 'leaf')  49.6 us
    all_to_all x4, blocking collectives, gram_apply(): lax.all_to_all(returned.reshape(leaves, sides * rank_size), 'leaf', split...  38.9 us
    psum x4, blocking collectives, gram_apply(): totals = lax.psum(partial_value, 'rows')  24.3 us
    all_to_all x2, blocking collectives, gram_apply(): lax.all_to_all(outgoing.reshape(leaves, sides * rank_size), 'leaf', split...  17.9 us
    scatter x8, local copies, waits for them, and re-layouts, gram_apply(): return jnp.zeros_like(tree_out).at[:, local_index].set(tree_out)  13.5 us
    gather x8, local copies, waits for them, and re-layouts, gram_apply(): taken_tree = jnp.take(field, local_index, axis=1).astype(jnp.bfloat16)  13.3 us
    all_to_all x2, starting transfers between devices, gram_apply(): lax.all_to_all(outgoing.reshape(leaves, sides * rank_size), 'leaf', split...  10.6 us
  transfers between devices with their start and end apart: 2, of which 2 were waited for; matrix products, arithmetic and copies ran while one was open for 0% of the time, Pallas kernels for 0%

profile of v1, /device:TPU:0, one launch (start us, length us, event | category | flops | bytes accessed | tf_op | source)
XLA Modules:
  0.0 282.6 jit_solution(3488124847591782563)
XLA Ops:
  9.9 7.3 %all-to-all-start = ((bf16[8,2,192]{2,1,0:T(2,128)(2,1)}), bf16[8,2,192]{2,1,0:T(2,128)(2,1)S(1)}, u32[]{:S(2)}, u32[]{:S(2)}) async-start(bf16[8,2,192]{2,1,0:T(2,128)(2,1)} %reshape.246), calls=%async_computation | async-start | bytes 16384 | tf_op jit(solution)/shard_map/all_to_all | solution.py:39
  17.5 5.3 %all-gather = f32[192,48]{1,0:T(8,128)S(1)} all-gather(f32[48,48]{1,0:T(8,128)S(1)} %fusion.74), channel_id=2, replica_groups=mesh['leaf'=8,'rows'=4] {'rows'}, dimensions={0}, use_global_device_ids=true | all-gather | bytes 46080 | tf_op jit(solution)/shard_map/all_gather | solution.py:29
  24.1 6.3 %psum.70 = bf16[8,192]{1,0:T(8,128)(2,1)S(1)} all-reduce(f32[8,192]{1,0:T(8,128)S(1)} %convolution_bitcast_fusion.7), channel_id=1, replica_groups=mesh['leaf'=8,'rows'=4] {'rows'}, use_global_device_ids=true, to_apply=%region_0.2 | all-reduce | flops 1536 | bytes 9216 | tf_op jit(solution)/shard_map/psum | solution.py:51
  31.9 12.3 %all_to_all.80 = bf16[8,2,192]{2,1,0:T(2,128)(2,1)S(1)} all-to-all(bf16[8,2,192]{2,1,0:T(2,128)(2,1)S(1)} %reshape.248), channel_id=1, replica_groups=mesh['leaf'=8,'rows'=4] {'leaf'}, dimensions={0} | all-to-all | bytes 12288 | tf_op jit(solution)/shard_map/all_to_all | solution.py:61
  45.0 3.2 %scatter_custom_fusion = f32[8,1024]{0,1:T(8,128)S(1)} fusion(s32[1024]{0:T(1024)S(1)} %get-tuple-element.14, f32[1024,8]{1,0:T(8,128)S(1)} %copy.180, f32[]{:T(128)} %constant.15.clone.1), kind=kCustom, calls=%fused_computation.54 | custom fusion | bytes 32772 | tf_op jit(solution)/shard_map/scatter | solution.py:73
  54.7 3.3 %all-to-all-start.2 = ((bf16[8,2,192]{2,1,0:T(2,128)(2,1)}), bf16[8,2,192]{2,1,0:T(2,128)(2,1)S(1)}, u32[]{:S(2)}, u32[]{:S(2)}) async-start(bf16[8,2,192]{2,1,0:T(2,128)(2,1)} %reshape.250), calls=%async_computation.2 | async-start | bytes 16384 | tf_op jit(solution)/shard_map/all_to_all | solution.py:39
  58.2 6.3 %all-to-all-done.2 = bf16[8,2,192]{2,1,0:T(2,128)(2,1)S(1)} async-done(((bf16[8,2,192]{2,1,0:T(2,128)(2,1)}), bf16[8,2,192]{2,1,0:T(2,128)(2,1)S(1)}, u32[]{:S(2)}, u32[]{:S(2)}) %all-to-all-start.2) | async-done | bytes 6176 | tf_op jit(solution)/shard_map/all_to_all | solution.py:39
  64.9 6.0 %psum.73 = bf16[8,192]{1,0:T(8,128)(2,1)S(1)} all-reduce(f32[8,192]{1,0:T(8,128)S(1)} %convolution_bitcast_fusion.6), channel_id=1, replica_groups=mesh['leaf'=8,'rows'=4] {'rows'}, use_global_device_ids=true, to_apply=%region_5.7 | all-reduce | flops 1536 | bytes 9216 | tf_op jit(solution)/shard_map/psum | solution.py:51
  72.3 8.9 %all_to_all.81 = bf16[8,2,192]{2,1,0:T(2,128)(2,1)S(1)} all-to-all(bf16[8,2,192]{2,1,0:T(2,128)(2,1)S(1)} %reshape.252), channel_id=1, replica_groups=mesh['leaf'=8,'rows'=4] {'leaf'}, dimensions={0} | all-to-all | bytes 12288 | tf_op jit(solution)/shard_map/all_to_all | solution.py:61
  82.0 3.2 %scatter_custom_fusion.1 = f32[8,1024]{0,1:T(8,128)S(1)} fusion(s32[1024]{0:T(1024)S(1)} %get-tuple-element.14, f32[1024,8]{1,0:T(8,128)S(1)} %copy.194, f32[]{:T(128)} %constant.15.clone.1), kind=kCustom, calls=%fused_computation.52 | custom fusion | bytes 32772 | tf_op jit(solution)/shard_map/scatter | solution.py:73
  85.6 5.8 %psum.71 = f32[8]{0:T(128)S(1)} all-reduce(f32[8]{0:T(128)S(1)} %get-tuple-element.12), channel_id=1, replica_groups=mesh['leaf'=8,'rows'=4] {'rows'}, use_global_device_ids=true, to_apply=%region_3.5 | all-reduce | flops 8 | bytes 64 | tf_op jit(solution)/shard_map/psum | solution.py:14
  91.4 38.2 %psum.74 = f32[8]{0:T(128)S(1)} all-reduce(f32[8]{0:T(128)S(1)} %get-tuple-element.11), channel_id=1, replica_groups=mesh['leaf'=8,'rows'=4] {'leaf','rows'}, use_global_device_ids=true, to_apply=%region_8.10 | all-reduce | flops 8 | bytes 64 | tf_op jit(solution)/shard_map/psum | solution.py:10
  129.5 20.4 %psum.72 = f32[8]{0:T(128)S(1)} all-reduce(f32[8]{0:T(128)S(1)} %psum.71), channel_id=1, replica_groups=mesh['leaf'=8,'rows'=4] {'leaf'}, use_global_device_ids=true, to_apply=%region_4.6 | all-reduce | flops 8 | bytes 64 | tf_op jit(solution)/shard_map/psum | solution.py:14
  155.1 8.9 %all_to_all.82 = bf16[8,2,192]{2,1,0:T(2,128)(2,1)S(1)} all-to-all(bf16[8,2,192]{2,1,0:T(2,128)(2,1)S(1)} %reshape.254), channel_id=1, replica_groups=mesh['leaf'=8,'rows'=4] {'leaf'}, dimensions={0} | all-to-all | bytes 12288 | tf_op jit(solution)/shard_map/all_to_all | solution.py:39
  164.4 6.1 %psum.75 = bf16[8,192]{1,0:T(8,128)(2,1)S(1)} all-reduce(f32[8,192]{1,0:T(8,128)S(1)} %convolution_bitcast_fusion.5), channel_id=1, replica_groups=mesh['leaf'=8,'rows'=4] {'rows'}, use_global_device_ids=true, to_apply=%region_9.11 | all-reduce | flops 1536 | bytes 9216 | tf_op jit(solution)/shard_map/psum | solution.py:51
  172.0 8.9 %all_to_all.83 = bf16[8,2,192]{2,1,0:T(2,128)(2,1)S(1)} all-to-all(bf16[8,2,192]{2,1,0:T(2,128)(2,1)S(1)} %reshape.256), channel_id=1, replica_groups=mesh['leaf'=8,'rows'=4] {'leaf'}, dimensions={0} | all-to-all | bytes 12288 | tf_op jit(solution)/shard_map/all_to_all | solution.py:61
  181.7 3.2 %scatter_custom_fusion.2 = f32[8,1024]{0,1:T(8,128)S(1)} fusion(s32[1024]{0:T(1024)S(1)} %get-tuple-element.14, f32[1024,8]{1,0:T(8,128)S(1)} %copy.207, f32[]{:T(128)} %constant.15.clone.1), kind=kCustom, calls=%fused_computation.50 | custom fusion | bytes 32772 | tf_op jit(solution)/shard_map/scatter | solution.py:73
  185.2 5.8 %psum.76 = f32[8]{0:T(128)S(1)} all-reduce(f32[8]{0:T(128)S(1)} %multiply_reduce_fusion.1), channel_id=1, replica_groups=mesh['leaf'=8,'rows'=4] {'rows'}, use_global_device_ids=true, to_apply=%region_12.14 | all-reduce | flops 8 | bytes 64 | tf_op jit(solution)/shard_map/psum | solution.py:14
  190.9 17.7 %psum.77 = f32[8]{0:T(128)S(1)} all-reduce(f32[8]{0:T(128)S(1)} %psum.76), channel_id=1, replica_groups=mesh['leaf'=8,'rows'=4] {'leaf'}, use_global_device_ids=true, to_apply=%region_13.15 | all-reduce | flops 8 | bytes 64 | tf_op jit(solution)/shard_map/psum | solution.py:14
  213.8 9.0 %all_to_all.84 = bf16[8,2,192]{2,1,0:T(2,128)(2,1)S(1)} all-to-all(bf16[8,2,192]{2,1,0:T(2,128)(2,1)S(1)} %reshape.258), channel_id=1, replica_groups=mesh['leaf'=8,'rows'=4] {'leaf'}, dimensions={0} | all-to-all | bytes 12288 | tf_op jit(solution)/shard_map/all_to_all | solution.py:39
  223.2 5.8 %psum.78 = bf16[8,192]{1,0:T(8,128)(2,1)S(1)} all-reduce(f32[8,192]{1,0:T(8,128)S(1)} %convolution_bitcast_fusion.4), channel_id=1, replica_groups=mesh['leaf'=8,'rows'=4] {'rows'}, use_global_device_ids=true, to_apply=%region_14.16 | all-reduce | flops 1536 | bytes 9216 | tf_op jit(solution)/shard_map/psum | solution.py:51
  230.5 8.9 %all_to_all.85 = bf16[8,2,192]{2,1,0:T(2,128)(2,1)S(1)} all-to-all(bf16[8,2,192]{2,1,0:T(2,128)(2,1)S(1)} %reshape.260), channel_id=1, replica_groups=mesh['leaf'=8,'rows'=4] {'leaf'}, dimensions={0} | all-to-all | bytes 12288 | tf_op jit(solution)/shard_map/all_to_all | solution.py:61
  240.2 3.2 %scatter_custom_fusion.3 = f32[8,1024]{0,1:T(8,128)S(1)} fusion(s32[1024]{0:T(1024)S(1)} %get-tuple-element.14, f32[1024,8]{1,0:T(8,128)S(1)} %copy.220, f32[]{:T(128)} %constant.15.clone.1), kind=kCustom, calls=%fused_computation.48 | custom fusion | bytes 32772 | tf_op jit(solution)/shard_map/scatter | solution.py:73
  243.7 38.2 %psum.79 = f32[8]{0:T(128)S(1)} all-reduce(f32[8]{0:T(128)S(1)} %multiply_reduce_fusion), channel_id=1, replica_groups=mesh['leaf'=8,'rows'=4] {'leaf','rows'}, use_global_device_ids=true, to_apply=%region_17.19 | all-reduce | flops 8 | bytes 64 | tf_op jit(solution)/shard_map/psum | solution.py:10
  (142 shorter events, 39.4 us)
Async XLA Ops:
  0.6 16.6 %copy-start = (bf16[48,1024]{1,0:T(8,128)(2,1)S(1)}, bf16[48,1024]{1,0:T(8,128)(2,1)}, u32[]{:S(2)}) copy-start(bf16[48,1024]{1,0:T(8,128)(2,1)} %param.17) | copy-start | bytes 294916
  7.1 0.7 copy-start.5
  7.9 9.4 %copy-start.3 = (bf16[384,192]{0,1:T(8,128)(2,1)S(1)}, bf16[384,192]{0,1:T(8,128)(2,1)}, u32[]{:S(2)}) copy-start(bf16[384,192]{0,1:T(8,128)(2,1)} %param.16) | copy-start | bytes 442372
  9.9 13.8 %all-to-all-start = ((bf16[8,2,192]{2,1,0:T(2,128)(2,1)}), bf16[8,2,192]{2,1,0:T(2,128)(2,1)S(1)}, u32[]{:S(2)}, u32[]{:S(2)}) async-start(bf16[8,2,192]{2,1,0:T(2,128)(2,1)} %reshape.246), calls=%async_computation | async-start | bytes 16384 | tf_op jit(solution)/shard_map/all_to_all | solution.py:39
  48.3 0.8 copy-start.1
  48.3 0.8 copy-start.2
  52.5 5.5 %copy-start.4 = (bf16[384,192]{0,1:T(8,128)(2,1)S(1)}, bf16[384,192]{0,1:T(8,128)(2,1)}, u32[]{:S(2)}) copy-start(bf16[384,192]{0,1:T(8,128)(2,1)} %param.15) | copy-start | bytes 442372
  54.7 9.8 %all-to-all-start.2 = ((bf16[8,2,192]{2,1,0:T(2,128)(2,1)}), bf16[8,2,192]{2,1,0:T(2,128)(2,1)S(1)}, u32[]{:S(2)}, u32[]{:S(2)}) async-start(bf16[8,2,192]{2,1,0:T(2,128)(2,1)} %reshape.250), calls=%async_computation.2 | async-start | bytes 16384 | tf_op jit(solution)/shard_map/all_to_all | solution.py:39
